TPU v7x, 32 devices: a whole 2x2x4 slice. The times are simulated.
32 devices in a mesh: blk: 4 (over x, core), group: 8 (over z, y).
Axes of the slice: x: 2, y: 2, z: 4, core: 2. Of those that a mesh axis runs over, the one named last changes fastest.
Arguments:
- queries: bfloat16 [8, 512, 2048], P('group', 'blk'), may hold values from -300 to 300
- normed: bfloat16 [8, 512, 2048], P('group', 'blk'), may hold values from -6 to 6
- key_weight_copies: bfloat16 [8, 2048, 512], P('group', 'blk'), may hold values from -0.125 to 0.125
- value_weight_copies: bfloat16 [8, 2048, 512], P('group', 'blk'), may hold values from -0.125 to 0.125
- owner: int32 [4], replicated, may hold values from 0 to 7
Outputs:
- cache_keys: bfloat16 [8, 512, 512], P('group', 'blk')
- cache_values: bfloat16 [8, 512, 512], P('group', 'blk')
- attended: bfloat16 [8, 512, 2048], P('group', 'blk')
Inputs may be any that keep to these rules, and one draw needn't show every extreme that they name: `owner`: learner group index of each block of projection rows, below the number of actor groups.
All inputs are finite; a program needn't handle non-finite values.
Results may differ from a plain program's by a relative error of at most 0.011.
Values may be sent and summed in bfloat16 or wider, within the bound.
A program may use at most 64 MiB of HBM per device.

v0:
```python
import math
import jax
import jax.numpy as jnp
from jax import lax
from jax.sharding import PartitionSpec as P

QUERY_HEADS = 16
KEY_VALUE_HEADS = 4
HEAD_SIZE = 128


def spread(value, axis, source):
    kept = jnp.where(lax.axis_index(axis) == source, value, 0).astype(value.dtype)
    return lax.psum(kept, axis)


def rotate(unshaped_rows, positions):
    half_dim = HEAD_SIZE // 2
    inverse_freq = jnp.exp(
        jnp.arange(half_dim).astype(jnp.float32) * (-2.0 * math.log(500000.0) / HEAD_SIZE)
    )
    angles = positions.astype(jnp.float32)[:, None] * inverse_freq[None, :]
    cos_table = jnp.cos(angles)[:, None, :]
    sin_table = jnp.sin(angles)[:, None, :]
    reshaped_rows = unshaped_rows.reshape(unshaped_rows.shape[0], KEY_VALUE_HEADS, HEAD_SIZE)
    first_half = reshaped_rows[..., :half_dim]
    second_half = reshaped_rows[..., half_dim:]
    transposed_rows = jnp.concatenate(
        [
            first_half * cos_table - second_half * sin_table,
            second_half * cos_table + first_half * sin_table,
        ],
        axis=-1,
    )
    return transposed_rows.reshape(unshaped_rows.shape[0], KEY_VALUE_HEADS * HEAD_SIZE)


def body(queries, normed, key_weight_copies, value_weight_copies, owner):
    input_rows = normed[0]
    token_rows = input_rows.shape[0]
    owner_group = lax.dynamic_index_in_dim(owner, lax.axis_index("blk"), 0, keepdims=False)
    shard_keys, shard_values = (
        spread(key_weight_copies[0], "group", owner_group),
        spread(value_weight_copies[0], "group", owner_group),
    )
    pieces = (
        lax.all_gather(shard_keys, "blk", axis=0, tiled=True),
        lax.all_gather(shard_values, "blk", axis=0, tiled=True),
    )
    key_raw = jnp.dot(input_rows, pieces[0], preferred_element_type=jnp.float32)
    value_raw = jnp.dot(input_rows, pieces[1], preferred_element_type=jnp.float32)
    positions = lax.axis_index("blk") * token_rows + jnp.arange(token_rows, dtype=jnp.int32)
    cache_keys = rotate(key_raw, positions).astype(jnp.bfloat16)
    cache_values = value_raw.astype(jnp.bfloat16)
    query_head_grid = queries[0].reshape(
        token_rows, KEY_VALUE_HEADS, QUERY_HEADS // KEY_VALUE_HEADS, HEAD_SIZE
    )
    score_scale = HEAD_SIZE ** (-0.5)
    start_state = (
        jnp.full((KEY_VALUE_HEADS, QUERY_HEADS // KEY_VALUE_HEADS, token_rows), -1e30, jnp.float32),
        jnp.zeros((KEY_VALUE_HEADS, QUERY_HEADS // KEY_VALUE_HEADS, token_rows), jnp.float32),
        jnp.zeros(
            (KEY_VALUE_HEADS, QUERY_HEADS // KEY_VALUE_HEADS, token_rows, HEAD_SIZE), jnp.float32
        ),
    )
    pieces = (
        lax.all_gather(cache_keys, "blk", axis=0, tiled=True),
        lax.all_gather(cache_values, "blk", axis=0, tiled=True),
    )
    key_count = pieces[0].shape[0]
    key_row_width = math.gcd(key_count, 512)

    def one_block(block_turn, state_in):
        row_top, row_total, weighted_values = state_in
        offset = block_turn * key_row_width
        key_part = lax.dynamic_slice_in_dim(pieces[0], offset, key_row_width, 0).reshape(
            key_row_width, KEY_VALUE_HEADS, HEAD_SIZE
        )
        value_part = lax.dynamic_slice_in_dim(pieces[1], offset, key_row_width, 0).reshape(
            key_row_width, KEY_VALUE_HEADS, HEAD_SIZE
        )
        scores = (
            jnp.einsum(
                "lewc,jec->ewlj", query_head_grid, key_part, preferred_element_type=jnp.float32
            )
            * score_scale
        )
        key_pos = offset + jnp.arange(key_row_width, dtype=jnp.int32)
        allowed = key_pos[None, :] <= positions[:, None]
        scores = jnp.where(allowed, scores, -jnp.inf)
        new_top = jnp.maximum(row_top, jnp.max(scores, axis=-1))
        fade_by = jnp.exp(row_top - new_top)
        prob_block = jnp.exp(scores - new_top[..., None])
        row_total = row_total * fade_by + jnp.sum(prob_block, axis=-1)
        weighted_values = weighted_values * fade_by[..., None] + jnp.einsum(
            "lxbp,plj->lxbj",
            prob_block.astype(jnp.bfloat16),
            value_part,
            preferred_element_type=jnp.float32,
        )
        return (new_top, row_total, weighted_values)

    row_top, row_total, weighted_values = lax.fori_loop(
        0, key_count // key_row_width, one_block, start_state
    )
    attended = (
        (weighted_values / row_total[..., None])
        .transpose(2, 0, 1, 3)
        .reshape(token_rows, QUERY_HEADS * HEAD_SIZE)
        .astype(jnp.bfloat16)
    )
    return (cache_keys[None], cache_values[None], attended[None])


def solution(mesh):
    placed = (
        P("group", "blk", None),
        P("group", "blk", None),
        P("group", "blk", None),
        P("group", "blk", None),
        P(),
    )
    return jax.shard_map(
        body,
        mesh=mesh,
        in_specs=placed,
        out_specs=(P("group", "blk", None), P("group", "blk", None), P("group", "blk", None)),
        check_vma=False,
    )
```

profile of v0, /device:TPU:0, one launch (start us, length us, event | category | flops | bytes accessed | tf_op | source)
XLA Modules:
  0.0 169.3 jit_solution(15250934654074469088)
XLA Ops:
  7.2 0.0 copy-start
  7.2 0.0 copy-start.1
  7.2 0.0 all-reduce.3.cloned.1.call-start
  7.2 1.3 dynamic_slice.8
  9.2 1.1 select_bitcast_fusion
  10.3 0.0 all-reduce.3.cloned.1.call-update
  10.3 0.0 all-gather.5.cloned.1.call-start
  10.4 82.8 %all-reduce.3.cloned.1.call-done = (bf16[512,512]{1,0:T(8,128)(2,1)}, bf16[512,512]{1,0:T(8,128)(2,1)}) async-done(((bf16[512,512]{1,0:T(8,128)(2,1)}, bf16[512,512]{1,0:T(8,128)(2,1)}), (bf16[512,512]{1,0:T(8,128)(2,1)}, bf16[512,512]{1,0:T(8,128)(2,1)})) %all-reduce.3.cloned.1.call-update) | async-done | bytes 1048592 | tf_op jit(solution)/shard_map/psum | solution.py:14
  93.1 0.0 all-gather.5.cloned.1.call-update
  93.2 0.0 all-gather.3.cloned.1.call-start
  93.2 0.7 all-gather.3.cloned.1.call-update
  93.9 0.0 copy-done.1
  93.9 0.4 reshape_squeeze.3
  94.4 0.2 multiply_cosine_fusion
  94.6 22.3 %all-gather.5.cloned.1.call-done = bf16[2048,512]{1,0:T(8,128)(2,1)} async-done(((bf16[512,512]{1,0:T(8,128)(2,1)}), bf16[2048,512]{1,0:T(8,128)(2,1)}) %all-gather.5.cloned.1.call-update) | async-done | bytes 2097168 | tf_op jit(solution)/shard_map/all_gather | solution.py:48
  116.9 0.0 copy-done
  116.9 2.3 %convolution_convert_fusion = bf16[512,128]{1,0:T(8,128)(2,1)S(1)} fusion(bf16[2048,512]{1,0:T(8,128)(2,1)} %all-gather.5.cloned.1.call-done, bf16[1,128,2048]{2,1,0:T(8,128)(2,1)S(1)} %copy-done), kind=kOutput, calls=%fused_computation.12 | convolution fusion | flops 268500992 | bytes 2752512 | tf_op jit(solution)/shard_map/dot_general | solution.py:51
  119.3 0.8 copy.17
  120.0 21.0 %all-gather.3.cloned.1.call-done = bf16[2048,512]{1,0:T(8,128)(2,1)} async-done(((bf16[512,512]{1,0:T(8,128)(2,1)}), bf16[2048,512]{1,0:T(8,128)(2,1)}) %all-gather.3.cloned.1.call-update) | async-done | bytes 2097168 | tf_op jit(solution)/shard_map/all_gather | solution.py:47
  141.1 2.3 %fusion.18 = f32[512,128]{1,0:T(8,128)S(1)} fusion(bf16[2048,512]{1,0:T(8,128)(2,1)} %all-gather.3.cloned.1.call-done, bf16[1,128,2048]{2,1,0:T(8,128)(2,1)S(1)} %copy-done), kind=kOutput, calls=%fused_computation.15 | convolution fusion | flops 268435456 | bytes 2883584 | tf_op jit(solution)/shard_map/dot_general | solution.py:50
  143.5 0.8 copy.22
  144.3 7.2 %all_gather.15 = bf16[512,512]{0,1:T(8,128)(2,1)S(1)} all-gather(bf16[128,512]{0,1:T(8,128)(2,1)S(1)} %bitcast.64), channel_id=1, replica_groups=mesh['blk'=4,'group'=8] {'blk'}, dimensions={0}, use_global_device_ids=true | all-gather | bytes 655360 | tf_op jit(solution)/shard_map/all_gather | solution.py:68
  151.4 7.3 %all_gather.14 = bf16[512,512]{0,1:T(8,128)(2,1)S(1)} all-gather(bf16[128,512]{0,1:T(8,128)(2,1)S(1)} %bitcast.62), channel_id=1, replica_groups=mesh['blk'=4,'group'=8] {'blk'}, dimensions={0}, use_global_device_ids=true | all-gather | bytes 655360 | tf_op jit(solution)/shard_map/all_gather | solution.py:67
  158.7 0.9 fusion.2
  159.6 0.9 fusion
  160.5 1.2 divide_convert_fusion
  161.7 1.0 copy.18
  (8 shorter events, 0.1 us)
Async XLA Ops:
  7.2 109.8 %copy-start = (bf16[1,128,2048]{2,1,0:T(8,128)(2,1)S(1)}, bf16[1,128,2048]{2,1,0:T(8,128)(2,1)}, u32[]{:S(2)}) copy-start(bf16[1,128,2048]{2,1,0:T(8,128)(2,1)} %param.6) | copy-start | bytes 1572868
  7.2 86.7 %copy-start.1 = (bf16[1,128,2048]{2,1,0:T(8,128)(2,1)S(1)}, bf16[1,128,2048]{2,1,0:T(8,128)(2,1)}, u32[]{:S(2)}) copy-start(bf16[1,128,2048]{2,1,0:T(8,128)(2,1)} %param.5) | copy-start | bytes 1572868
  7.2 86.0 %all-reduce.3.cloned.1.call-start = ((), (), s32[]{:S(2)}) async-start(), calls=%async_computation.2 | async-start | bytes 2097152 | tf_op jit(solution)/shard_map/psum | solution.py:14
  10.3 106.6 %all-gather.5.cloned.1.call-start = ((), (), s32[]{:S(2)}) async-start(), calls=%async_computation.1 | async-start | bytes 2621440 | tf_op jit(solution)/shard_map/all_gather | solution.py:48
  93.2 47.9 %all-gather.3.cloned.1.call-start = ((), (), s32[]{:S(2)}) async-start(), calls=%async_computation | async-start | bytes 2621440 | tf_op jit(solution)/shard_map/all_gather | solution.py:47
Sparse Core Ops, SparseCore 0:
  12.1 80.9 all-reduce.2
  94.7 22.1 all-gather.4
  118.5 22.5 all-gather.2
where the time goes:
time: 169 us
  waiting for transfers between devices  127 us (75%)
  blocking collectives  14.5 us (9%)
  between operations  14.5 us (9%)
  matrix products  6.72 us (4%)
  local copies, waits for them, and re-layouts  4.27 us (3%)
  other arithmetic  2.28 us (1%)
    psum x1, waiting for transfers between devices, spread(): return lax.psum(kept, axis)  82.8 us
    all_gather x1, waiting for transfers between devices, body(): lax.all_gather(shard_values, 'blk', axis=0, tiled=True)  22.3 us
    all_gather x1, waiting for transfers between devices, body(): lax.all_gather(shard_keys, 'blk', axis=0, tiled=True)  21 us
    all_gather x1, blocking collectives, body(): lax.all_gather(cache_keys, 'blk', axis=0, tiled=True)  7.29 us
    all_gather x1, blocking collectives, body(): lax.all_gather(cache_values, 'blk', axis=0, tiled=True)  7.18 us
  transfers between devices with their start and end apart: 3, of which 3 were waited for; matrix products, arithmetic and copies ran while one was open for 2% of the time, Pallas kernels for 0%

commit v1 on v0

--- a/solution.py
+++ b/solution.py
@@ -11,7 +11,7 @@
 
 def spread(value, axis, source):
     kept = jnp.where(lax.axis_index(axis) == source, value, 0).astype(value.dtype)
-    return lax.psum(kept, axis)
+    return jnp.sum(lax.all_gather(kept, axis), axis=0)
 
 
 def rotate(unshaped_rows, positions):

time: 169 us -> 235 us (1.39)
  waiting for transfers between devices: 127 us -> 185 us
  other arithmetic: 2.28 us -> 10.4 us
    all_gather x0 -> x2, waiting for transfers between devices: none -> 145 us  [spread(): return jnp.sum(lax.all_gather(kept, axis), axis=0)]
    psum x1 -> x0, waiting for transfers between devices: 82.8 us -> none  [spread(): return lax.psum(kept, axis)]
    reduce_sum x0 -> x2, other arithmetic: none -> 7.47 us  [spread(): return jnp.sum(lax.all_gather(kept, axis), axis=0)]
  transfers between devices with their start and end apart: 3 -> 4, of which waited for: 3 -> 4; matrix products, arithmetic and copies ran while one was open for 2% -> 5% of each run, Pallas kernels for 0% -> 0%
where the time goes in v1:
time: 235 us
  waiting for transfers between devices  185 us (79%)
  blocking collectives  14.5 us (6%)
  between operations  14.5 us (6%)
  other arithmetic  10.4 us (4%)
  matrix products  6.72 us (3%)
  local copies, waits for them, and re-layouts  4.22 us (2%)
    all_gather x2, waiting for transfers between devices, spread(): return jnp.sum(lax.all_gather(kept, axis), axis=0)  145 us
    all_gather x1, waiting for transfers between devices, body(): lax.all_gather(shard_values, 'blk', axis=0, tiled=True)  20.8 us
    all_gather x1, waiting for transfers between devices, body(): lax.all_gather(shard_keys, 'blk', axis=0, tiled=True)  18.8 us
    reduce_sum x2, other arithmetic, spread(): return jnp.sum(lax.all_gather(kept, axis), axis=0)  7.47 us
    all_gather x1, blocking collectives, body(): lax.all_gather(cache_keys, 'blk', axis=0, tiled=True)  7.29 us
    all_gather x1, blocking collectives, body(): lax.all_gather(cache_values, 'blk', axis=0, tiled=True)  7.18 us
  transfers between devices with their start and end apart: 4, of which 4 were waited for; matrix products, arithmetic and copies ran while one was open for 5% of the time, Pallas kernels for 0%

profile of v1, /device:TPU:0, one launch (start us, length us, event | category | flops | bytes accessed | tf_op | source)
XLA Modules:
  0.0 235.1 jit_solution(17581424227489117133)
XLA Ops:
  7.2 0.0 copy-start
  7.2 0.0 all-gather.5.cloned.1.call-start
  7.2 1.3 dynamic_slice.8
  9.2 0.8 broadcast_select_fusion.1
  10.0 0.0 all-gather.5.cloned.1.call-update
  10.0 0.0 all-gather.9.cloned.1.call-start
  10.1 0.9 broadcast_select_fusion
  11.0 0.0 all-gather.9.cloned.1.call-update
  11.0 0.0 copy-start.1
  11.0 0.0 all-gather.7.cloned.1.call-start
  11.1 75.2 %all-gather.5.cloned.1.call-done = bf16[8,512,512]{2,1,0:T(8,128)(2,1)} async-done(((bf16[1,512,512]{2,1,0:T(8,128)(2,1)}), bf16[8,512,512]{2,1,0:T(8,128)(2,1)}) %all-gather.5.cloned.1.call-update) | async-done | bytes 4194320 | tf_op jit(solution)/shard_map/all_gather | solution.py:14
  86.2 3.7 %reduce_sum.36 = bf16[512,512]{1,0:T(8,128)(2,1)} reduce(bf16[8,512,512]{2,1,0:T(8,128)(2,1)} %all-gather.5.cloned.1.call-done, bf16[]{:T(256)} %constant.38.clone.1), dimensions={0}, to_apply=%region_0.1 | reduce | flops 1835008 | bytes 4718594 | tf_op jit(solution)/shard_map/reduce_sum | solution.py:14
  90.0 0.0 all-gather.7.cloned.1.call-update
  90.0 0.0 all-gather.11.cloned.1.call-start
  90.0 69.7 %all-gather.9.cloned.1.call-done = bf16[8,512,512]{2,1,0:T(8,128)(2,1)} async-done(((bf16[1,512,512]{2,1,0:T(8,128)(2,1)}), bf16[8,512,512]{2,1,0:T(8,128)(2,1)}) %all-gather.9.cloned.1.call-update) | async-done | bytes 4194320 | tf_op jit(solution)/shard_map/all_gather | solution.py:14
  159.7 3.7 %reduce_sum.37 = bf16[512,512]{1,0:T(8,128)(2,1)} reduce(bf16[8,512,512]{2,1,0:T(8,128)(2,1)} %all-gather.9.cloned.1.call-done, bf16[]{:T(256)} %constant.38.clone.1), dimensions={0}, to_apply=%region_1.2 | reduce | flops 1835008 | bytes 4718594 | tf_op jit(solution)/shard_map/reduce_sum | solution.py:14
  163.5 0.0 all-gather.11.cloned.1.call-update
  163.5 0.0 copy-done.1
  163.5 0.4 reshape_squeeze.3
  164.0 0.2 multiply_cosine_fusion
  164.2 18.8 %all-gather.7.cloned.1.call-done = bf16[2048,512]{1,0:T(8,128)(2,1)} async-done(((bf16[512,512]{1,0:T(8,128)(2,1)}), bf16[2048,512]{1,0:T(8,128)(2,1)}) %all-gather.7.cloned.1.call-update) | async-done | bytes 2097168 | tf_op jit(solution)/shard_map/all_gather | solution.py:47
  183.0 0.0 copy-done
  183.0 2.3 fusion.18
  185.4 0.8 copy.28
  186.2 20.8 %all-gather.11.cloned.1.call-done = bf16[2048,512]{1,0:T(8,128)(2,1)} async-done(((bf16[512,512]{1,0:T(8,128)(2,1)}), bf16[2048,512]{1,0:T(8,128)(2,1)}) %all-gather.11.cloned.1.call-update) | async-done | bytes 2097168 | tf_op jit(solution)/shard_map/all_gather | solution.py:48
  207.0 2.3 convolution_convert_fusion
  209.3 0.8 copy.23
  210.1 7.2 %all_gather.25 = bf16[512,512]{0,1:T(8,128)(2,1)S(1)} all-gather(bf16[128,512]{0,1:T(8,128)(2,1)S(1)} %bitcast.60), channel_id=1, replica_groups=mesh['blk'=4,'group'=8] {'blk'}, dimensions={0}, use_global_device_ids=true | all-gather | bytes 655360 | tf_op jit(solution)/shard_map/all_gather | solution.py:68
  217.3 7.3 %all_gather.24 = bf16[512,512]{0,1:T(8,128)(2,1)S(1)} all-gather(bf16[128,512]{0,1:T(8,128)(2,1)S(1)} %bitcast.58), channel_id=1, replica_groups=mesh['blk'=4,'group'=8] {'blk'}, dimensions={0}, use_global_device_ids=true | all-gather | bytes 655360 | tf_op jit(solution)/shard_map/all_gather | solution.py:67
  224.6 0.9 fusion.2
  225.5 0.9 fusion
  226.4 1.2 divide_convert_fusion
  227.6 1.0 copy.24
  (8 shorter events, 0.1 us)
Async XLA Ops:
  7.2 175.8 %copy-start = (bf16[1,128,2048]{2,1,0:T(8,128)(2,1)S(1)}, bf16[1,128,2048]{2,1,0:T(8,128)(2,1)}, u32[]{:S(2)}) copy-start(bf16[1,128,2048]{2,1,0:T(8,128)(2,1)} %param.6) | copy-start | bytes 1572868
  7.2 79.1 %all-gather.5.cloned.1.call-start = ((), (), s32[]{:S(2)}) async-start(), calls=%async_computation | async-start | bytes 4718592 | tf_op jit(solution)/shard_map/all_gather | solution.py:14
  10.0 149.7 %all-gather.9.cloned.1.call-start = ((), (), s32[]{:S(2)}) async-start(), calls=%async_computation.2 | async-start | bytes 4718592 | tf_op jit(solution)/shard_map/all_gather | solution.py:14
  11.0 152.5 %copy-start.1 = (bf16[1,128,2048]{2,1,0:T(8,128)(2,1)S(1)}, bf16[1,128,2048]{2,1,0:T(8,128)(2,1)}, u32[]{:S(2)}) copy-start(bf16[1,128,2048]{2,1,0:T(8,128)(2,1)} %param.5) | copy-start | bytes 1572868
  11.0 172.0 %all-gather.7.cloned.1.call-start = ((), (), s32[]{:S(2)}) async-start(), calls=%async_computation.1 | async-start | bytes 2621440 | tf_op jit(solution)/shard_map/all_gather | solution.py:47
  90.0 117.0 %all-gather.11.cloned.1.call-start = ((), (), s32[]{:S(2)}) async-start(), calls=%async_computation.3 | async-start | bytes 2621440 | tf_op jit(solution)/shard_map/all_gather | solution.py:48
Sparse Core Ops, SparseCore 0:
  10.7 75.5 all-gather.4
  88.4 71.3 all-gather.8
  161.9 21.0 all-gather.6
  184.4 22.5 all-gather.10
